TPU v7x, 32 devices: a whole 2x2x4 slice. The times are simulated.
32 devices in a mesh: role: 2 (over core), ctx: 2 (over y), req: 8 (over z, x).
Axes of the slice: x: 2, y: 2, z: 4, core: 2. Of those that a mesh axis runs over, the one named last changes fastest.
Arguments:
- cache: bfloat16 [16, 8192, 576], P(None, ('ctx', 'req'), 'role'), may hold values from -8 to 8
- lengths: int32 [16], replicated, may hold values from 2 to 8192
- request_decode_slot: int32 [16], replicated, may hold values from 0 to 15, as said below
- q_nope: bfloat16 [16, 4, 16384], P('req', None, ('role', 'ctx')), may hold values from -6 to 6
- q_rope: bfloat16 [16, 4, 8192], P('req', None, ('role', 'ctx')), may hold values from -8 to 8
- new_latent: bfloat16 [16, 4, 576], P('req'), may hold values from -4.1875 to 4.1875
- w_key: bfloat16 [128, 128, 512], P(('role', 'ctx')), may hold values from -0.5 to 0.5
- value_up_weight: bfloat16 [128, 512, 128], P(('role', 'ctx')), may hold values from -1 to 1
Outputs:
- attended: bfloat16 [16, 4, 16384], P('req', None, ('role', 'ctx'))
Inputs may be any that keep to these rules, and one draw needn't show every extreme that they name: A permutation of the slots; request r is owned by req index request_decode_slot[r] // 2.
All inputs are finite; a program needn't handle non-finite values.
Results may differ from a plain program's by a relative error of at most 0.007.
Values may be sent and summed in bfloat16 or wider, within the bound.
A program may use at most 128 MiB of HBM per device.

v0:
```python
import functools
import math

import jax
import jax.numpy as jnp
from jax import lax
from jax.experimental import pallas as pl
from jax.experimental.pallas import tpu as pltpu
from jax.sharding import PartitionSpec as P

NEG = -1e30
LOW = -1e29
MESH = pl.DeviceIdType.MESH
BLOCK_HEADS = 4


def xor_bit(value, bit, flip):
    b = lax.rem(lax.div(value, bit), 2)
    return value + flip * bit * (1 - 2 * b)


def owner_of(cl, k, chip):
    if cl == 0:
        return lax.rem(chip, 4) + 4 * k
    if cl == 1:
        return lax.rem(chip, 2) + 2 * lax.rem(k, 2) + 8 * lax.div(k, 2)
    return lax.rem(k, 2) + 2 * lax.rem(lax.div(chip, 2), 2) + 4 + 8 * lax.div(k, 2)


def neighbour(cl, p, chip):
    if cl == 0:
        return xor_bit(xor_bit(chip, 1, p % 2), 2, p // 2)
    return xor_bit(chip, cl, p)


def kernel(dims, inv_ref, len_ref, cache_ref, qn_ref, qr_ref, new_ref, wk_ref, vu_ref, out_ref,
           cache_v, ksend, k_a, k_b, wk_v, vu_v, rawn, rawr, qa, q_in, r_in, s_buf, m_buf, l_buf, acc,
           o_out, e_out, o_in, e_in, merged, att_out, f_out, att_a, f_a, att_b, f_b,
           load_sem, raw_ss, raw_rs, k_ss, ka_rs, kb_rs, q_ss, q_rs, o_ss, o_rs, t_ss, ta_rs, tb_rs):
    n_req, n_ctx, steps, scale2 = dims
    role, ctx, req = lax.axis_index("role"), lax.axis_index("ctx"), lax.axis_index("req")
    per = n_req // 8
    two = 2 * per
    high = n_req // 4
    total, half, span = cache_ref.shape
    heads, nope, latent = wk_ref.shape
    rows = heads * steps
    low, hi = lax.rem(req, 4), lax.div(req, 4)
    bit2 = lax.rem(hi, 2)
    other = 1 - role

    def role_at(rr):
        return role if rr == 0 else other

    def ctx_at(t):
        return lax.rem(ctx + t, n_ctx)

    loads = [pltpu.make_async_copy(cache_ref, cache_v, load_sem.at[0]),
             pltpu.make_async_copy(wk_ref, wk_v, load_sem.at[1]),
             pltpu.make_async_copy(vu_ref, vu_v, load_sem.at[2])]
    loads[0].start()
    loads[1].start()

    partners = []
    for d in (1, 2, 3):
        for rr in (0, 1):
            partners.append((role_at(rr), ctx, neighbour(0, d, req)))
    for t in range(n_ctx):
        for rr in (0, 1):
            if t or rr:
                partners.append((role_at(rr), ctx_at(t), req))
    for v in range(1, high):
        far = 4 * lax.rem(hi + v, high)
        for d in (0, 1, 2):
            partners.append((role, ctx, neighbour(0, d, low) + far))
    barrier = pltpu.get_barrier_semaphore()
    for dev in partners:
        pl.semaphore_signal(barrier, inc=1, device_id=dev, device_id_type=MESH)
    pl.semaphore_wait(barrier, len(partners))

    started = []

    def send(src, dst, ss, rs, dev):
        copy = pltpu.make_async_remote_copy(src_ref=src, dst_ref=dst, send_sem=ss, recv_sem=rs, device_id=dev,
                                            device_id_type=MESH)
        copy.start()
        started.append(copy)

    def arrived(ref, sem):
        pltpu.make_async_copy(ref, ref, sem).wait()

    mine_b = (1 + bit2) * two + lax.rem(lax.div(req, 2 - bit2), 2) * 0
    kk = jnp.where(bit2 == 0, lax.rem(lax.div(req, 2), 2), lax.rem(req, 2)) + 2 * lax.div(req, 8)
    mine_b = (1 + bit2) * two + kk
    mine_a = hi
    low_b = jnp.where(bit2 == 0, xor_bit(low, 2, 1), xor_bit(low, 1, 1))
    index = 0
    for slot, spot, dests in (
        (1, mine_b, [(u, v) for v in range(high) for u in (0, 1) if u or v]),
        (0, mine_a, [(0, v) for v in range(1, high)]),
    ):
        for u, v in dests:
            chip = (low_b if u else low) + 4 * lax.rem(hi + v, high)
            dev = (role, ctx, chip)
            send(qn_ref.at[slot], rawn.at[spot], raw_ss.at[index, 0], raw_rs.at[spot, 0], dev)
            send(qr_ref.at[slot], rawr.at[spot], raw_ss.at[index, 1], raw_rs.at[spot, 1], dev)
            index += 1
        rawn[spot] = qn_ref[slot]
        rawr[spot] = qr_ref[slot]

    loads[0].wait()
    loads[2].start()

    def k_ref(cl, m, p):
        return k_a.at[m, p] if cl == 0 else k_b.at[(cl - 1) * per + m, p]

    def k_sem(cl, m, p, h):
        return ka_rs.at[m, p, h] if cl == 0 else kb_rs.at[(cl - 1) * per + m, p, h]

    mine_rows = pl.ds(pl.multiple_of(role * half, 16), half)
    sends = []
    order = [(1, 1), (2, 1), (1, 0), (2, 0), (0, 1), (0, 2), (0, 3), (0, 0)]
    for cl, p in order:
        for rr in (0, 1):
            for m in range(per):
                sends.append((cl, p, rr, m))
    pending = None
    chunk = 0
    for cl, p, rr, m in sends:
        chip = neighbour(cl, p, req)
        slot = 2 * owner_of(cl, 2 * m + role_at(rr), chip) + (1 if cl else 0)
        data = cache_v[inv_ref[slot]]
        dst = k_ref(cl, m, p)
        if p == 0 and rr == 0:
            dst[mine_rows, :] = data
            continue
        ksend[chunk] = data
        if pending is not None:
            send(*pending)
        pending = (ksend.at[chunk], dst.at[mine_rows, :], k_ss.at[chunk], k_sem(cl, m, p, role),
                   (role_at(rr), ctx, chip))
        chunk += 1
    send(*pending)

    loads[1].wait()
    block = BLOCK_HEADS * steps
    lhs_rows = lax.broadcasted_iota(jnp.int32, (two * block, BLOCK_HEADS * nope), 0)
    lhs_cols = lax.broadcasted_iota(jnp.int32, (two * block, BLOCK_HEADS * nope), 1)
    diagonal = (lax.div(lax.rem(lhs_rows, block), steps) == lax.div(lhs_cols, nope)).astype(jnp.float32)
    diagonal = diagonal.astype(jnp.bfloat16)

    qcount = 0
    for cl in (1, 2, 0):
        for k in range(two):
            @pl.when(owner_of(cl, jnp.int32(k), req) != req)
            def _():
                arrived(rawn.at[cl * two + k], raw_rs.at[cl * two + k, 0])
                arrived(rawr.at[cl * two + k], raw_rs.at[cl * two + k, 1])

        def absorb(hb, carry):
            r0 = pl.multiple_of(hb * block, block)
            lhs = jnp.concatenate([rawn[cl * two + k, pl.ds(r0, block), :] for k in range(two)], axis=0)
            lhs = jnp.concatenate([lhs] * BLOCK_HEADS, axis=1) * diagonal
            w = wk_v[pl.ds(hb * BLOCK_HEADS, BLOCK_HEADS)].reshape(BLOCK_HEADS * nope, latent)
            res = jnp.dot(lhs, w, preferred_element_type=jnp.float32).astype(jnp.bfloat16)
            for k in range(two):
                qa[cl * two + k, pl.ds(r0, block), :] = res[k * block:(k + 1) * block]
            return carry

        lax.fori_loop(0, heads // BLOCK_HEADS, absorb, 0)
        for t in list(range(1, n_ctx)) + [0]:
            for rr in (0, 1):
                for m in range(per):
                    if t == 0 and rr == 0:
                        continue
                    k = cl * two + 2 * m + role_at(rr)
                    at = ((n_ctx - t) % n_ctx) * 2 + rr
                    dev = (role_at(rr), ctx_at(t), req)
                    send(rawr.at[k], r_in.at[cl * per + m, at], q_ss.at[qcount, 1], q_rs.at[cl * per + m, at, 1], dev)
                    send(qa.at[k], q_in.at[cl * per + m, at], q_ss.at[qcount, 0], q_rs.at[cl * per + m, at, 0], dev)
                    qcount += 1

    ocount = 0
    for cl in (1, 2, 0):
        parts = 4 if cl == 0 else 2
        for m in range(per):
            sl = cl * per + m
            owner = owner_of(cl, 2 * m + role, req)
            slot = 2 * owner + (1 if cl else 0)
            length = len_ref[inv_ref[slot]]
            fresh_on = jnp.logical_and(owner == req, ctx == 0)
            for nth, rel in enumerate(list(range(1, n_ctx)) + [0]):
                for rr in (0, 1):
                    if rel or rr:
                        arrived(q_in.at[sl, rel * 2 + rr], q_rs.at[sl, rel * 2 + rr, 0])
                        arrived(r_in.at[sl, rel * 2 + rr], q_rs.at[sl, rel * 2 + rr, 1])
                if rel == 0:
                    q_own, r_own = qa[cl * two + 2 * m + role], rawr[cl * two + 2 * m + role]
                else:
                    q_own, r_own = q_in[sl, rel * 2], r_in[sl, rel * 2]
                q = jnp.concatenate([q_own, q_in[sl, rel * 2 + 1]], axis=0)
                qr = jnp.concatenate([r_own.astype(jnp.float32).T, r_in[sl, rel * 2 + 1].astype(jnp.float32).T],
                                     axis=0).astype(jnp.bfloat16)
                new = new_ref[1 if cl else 0]
                nt = (((1,), (1,)), ((), ()))
                fresh = (lax.dot_general(q, new[:, :latent], nt, preferred_element_type=jnp.float32)
                         + lax.dot_general(qr, new[:, latent:], nt, preferred_element_type=jnp.float32)) * scale2
                token = lax.broadcasted_iota(jnp.int32, fresh.shape, 1)
                step = lax.rem(lax.broadcasted_iota(jnp.int32, fresh.shape, 0), steps)
                last = jnp.where(fresh_on, step, -1)
                fresh = jnp.where(token <= last, fresh, NEG)
                m_buf[...] = jnp.broadcast_to(jnp.max(fresh, axis=1, keepdims=True), m_buf.shape)

                def score(p, carry):
                    if nth == 0:
                        @pl.when(p > 0)
                        def _():
                            arrived(k_ref(cl, m, 0).at[pl.ds(0, half), :], k_sem(cl, m, p, role))
                        arrived(k_ref(cl, m, 0).at[pl.ds(0, half), :], k_sem(cl, m, p, other))
                    kk_ = k_ref(cl, m, p)
                    s = jnp.dot(q, kk_[:latent, :], preferred_element_type=jnp.float32)
                    s += jnp.dot(qr, kk_[latent:, :], preferred_element_type=jnp.float32)
                    if cl == 0:
                        chip = xor_bit(xor_bit(req, 1, lax.rem(p, 2)), 2, lax.div(p, 2))
                    else:
                        chip = xor_bit(req, cl, p)
                    first = (ctx * n_req + chip) * span
                    position = first + lax.broadcasted_iota(jnp.int32, (1, span), 1)
                    s = jnp.where(position < length, s * scale2, NEG)
                    s_buf[p] = s
                    m_buf[...] = jnp.maximum(m_buf[...], jnp.max(s, axis=1, keepdims=True))
                    return carry

                lax.fori_loop(0, parts, score, 0)
                top = jnp.maximum(m_buf[:, :1], LOW)
                weights = jnp.exp2(fresh - top)
                l_buf[...] = jnp.broadcast_to(jnp.sum(weights, axis=1, keepdims=True), l_buf.shape)
                acc[...] = jnp.dot(weights.astype(jnp.bfloat16), new[:, :latent], preferred_element_type=jnp.float32)

                def weigh(p, carry):
                    w = jnp.exp2(s_buf[p] - jnp.maximum(m_buf[:, :1], LOW))
                    l_buf[...] += jnp.sum(w, axis=1, keepdims=True)
                    acc[...] += lax.dot_general(w.astype(jnp.bfloat16), k_ref(cl, m, p)[:latent, :], nt,
                                                preferred_element_type=jnp.float32)
                    return carry

                lax.fori_loop(0, parts, weigh, 0)
                norm = l_buf[:, :1]
                live = norm > 0.0
                safe = jnp.where(live, norm, 1.0)
                o = (acc[...] * (1.0 / safe)).astype(jnp.bfloat16)
                lse = jnp.where(live, top + jnp.log2(safe), NEG)
                lse = jnp.broadcast_to(lse, (2 * rows, 128))
                k = cl * two + 2 * m + role
                back = (n_ctx - rel) % n_ctx
                for rr in (0, 1):
                    piece = o[rr * rows:(rr + 1) * rows]
                    e = lse[rr * rows:(rr + 1) * rows].T[:8]
                    if rel == 0 and rr == 0:
                        o_in[k, 0] = piece
                        e_in[k, 0] = e
                        continue
                    o_out[sl, rel * 2 + rr] = piece
                    e_out[sl, rel * 2 + rr] = e
                    dev = (role_at(rr), ctx_at(rel), req)
                    send(e_out.at[sl, rel * 2 + rr], e_in.at[k, back], o_ss.at[ocount, 1], o_rs.at[k, back, 1], dev)
                    send(o_out.at[sl, rel * 2 + rr], o_in.at[k, back], o_ss.at[ocount, 0], o_rs.at[k, back, 0], dev)
                    ocount += 1

    loads[2].wait()
    out_rows = lax.broadcasted_iota(jnp.int32, (two * block, 128), 0)
    which = lax.div(lax.rem(out_rows, block), steps)
    guarded = []
    for cl in (1, 2, 0):
        for rr in (0, 1):
            for m in range(per):
                k = cl * two + 2 * m + role_at(rr)
                for rel in range(n_ctx):
                    if rr or rel:
                        arrived(o_in.at[k, rel], o_rs.at[k, rel, 0])
                        arrived(e_in.at[k, rel], o_rs.at[k, rel, 1])
                es = [e_in[k, rel] for rel in range(n_ctx)]
                top = functools.reduce(jnp.maximum, es)
                shares = [jnp.exp2(e - top) for e in es]
                norm = sum(shares)
                f_out[k] = top + jnp.log2(norm)
                value = 0.0
                for rel in range(n_ctx):
                    w = jnp.broadcast_to((shares[rel] / norm)[:1], (128, rows)).T
                    w = jnp.concatenate([w] * (latent // 128), axis=1)
                    value = value + o_in[k, rel].astype(jnp.float32) * w
                merged[k] = value.astype(jnp.bfloat16)

        def up(hb, carry):
            r0 = pl.multiple_of(hb * block, block)
            lhs = jnp.concatenate([merged[cl * two + k, pl.ds(r0, block), :] for k in range(two)], axis=0)
            res = jnp.zeros((two * block, 128), jnp.float32)
            for j in range(BLOCK_HEADS):
                one = jnp.dot(lhs, vu_v[hb * BLOCK_HEADS + j], preferred_element_type=jnp.float32)
                res = jnp.where(which == j, one, res)
            res = res.astype(jnp.bfloat16)
            for k in range(two):
                att_out[cl * two + k, pl.ds(r0, block), :] = res[k * block:(k + 1) * block]
            return carry

        lax.fori_loop(0, heads // BLOCK_HEADS, up, 0)
        for k in range(two):
            e = cl * two + k
            owner = owner_of(cl, jnp.int32(k), req)
            if cl == 0:
                at, dst, fdst, sems = hi, att_a, f_a, ta_rs
            elif cl == 1:
                at, dst, fdst, sems = lax.div(req, 2), att_b, f_b, tb_rs
            else:
                at, dst, fdst, sems = lax.rem(req, 2) + 2 * hi, att_b, f_b, tb_rs
            copies = [
                pltpu.make_async_remote_copy(
                    src_ref=src.at[e], dst_ref=d.at[at], send_sem=t_ss.at[e, j], recv_sem=sems.at[at, j],
                    device_id=(role, ctx, owner), device_id_type=MESH)
                for j, (src, d) in enumerate(((att_out, dst), (f_out, fdst)))
            ]

            @pl.when(owner != req)
            def _():
                for copy in copies:
                    copy.start()

            @pl.when(owner == req)
            def _():
                dst[at] = att_out[e]
                fdst[at] = f_out[e]
            guarded.append((owner, copies))

    own_b = jnp.where(bit2 == 0, lax.div(req, 2), lax.rem(req, 2) + 2 * hi)
    for slot, count, src, fsrc, sems, own in ((1, 4 * per, att_b, f_b, tb_rs, own_b), (0, high, att_a, f_a, ta_rs, hi)):
        for j in range(count):
            @pl.when(own != j)
            def _():
                arrived(src.at[j], sems.at[j, 0])
                arrived(fsrc.at[j], sems.at[j, 1])
        es = [fsrc[j] for j in range(count)]
        top = functools.reduce(jnp.maximum, es)
        shares = [jnp.exp2(e - top) for e in es]
        norm = sum(shares)
        value = 0.0
        for j in range(count):
            w = jnp.broadcast_to((shares[j] / norm)[:1], (128, rows)).T
            value = value + src[j].astype(jnp.float32) * w
        out_ref[slot] = value.astype(jnp.bfloat16)

    for copy in started:
        copy.wait_send()
    for owner, copies in guarded:
        @pl.when(owner != req)
        def _():
            for copy in copies:
                copy.wait_send()


def shards(cache, lengths, request_decode_slot, q_nope, q_rope, new_latent, w_key, value_up_weight):
    total = request_decode_slot.shape[0]
    n_req, n_ctx = lax.axis_size("req"), lax.axis_size("ctx")
    heads, nope, latent = w_key.shape
    vdim = value_up_weight.shape[2]
    own, steps = q_nope.shape[:2]
    rope = q_rope.shape[2] // heads
    span, half = cache.shape[1:]
    rows = heads * steps
    per, two, high = n_req // 8, n_req // 4, n_req // 4
    groups = 2 * n_ctx
    scale2 = (nope + rope) ** (-0.5) * math.log2(math.e)

    slots = jnp.arange(total, dtype=jnp.int32)
    inverse = jnp.sum(
        jnp.where(request_decode_slot[None, :] == slots[:, None], slots[None, :], 0), axis=1
    ).astype(jnp.int32)
    turned = jnp.swapaxes(cache, 1, 2)
    qn = q_nope.reshape(own, steps, heads, nope).swapaxes(1, 2).reshape(own, rows, nope)
    qr = q_rope.reshape(own, steps, heads, rope).transpose(0, 3, 2, 1).reshape(own, rope, rows)
    new = jnp.pad(new_latent, ((0, 0), (0, 128 - steps), (0, 0)))
    bf, f32 = jnp.bfloat16, jnp.float32
    chunks = total - 3 * per
    vm, dma = pltpu.VMEM, pltpu.SemaphoreType.DMA
    smem = pl.BlockSpec(memory_space=pltpu.SMEM)
    here = pl.BlockSpec(memory_space=pltpu.VMEM)
    away = pl.BlockSpec(memory_space=pl.ANY)
    out = pl.pallas_call(
        functools.partial(kernel, (n_req, n_ctx, steps, scale2)),
        out_shape=jax.ShapeDtypeStruct((own, rows, vdim), bf),
        in_specs=[smem, smem, away, here, here, here, away, away],
        out_specs=here,
        scratch_shapes=[
            vm((total, half, span), bf),
            vm((chunks, half, span), bf),
            vm((per, 4, 2 * half, span), bf),
            vm((2 * per, 2, 2 * half, span), bf),
            vm(w_key.shape, bf),
            vm(value_up_weight.shape, bf),
            vm((3 * two, rows, nope), bf),
            vm((3 * two, rope, rows), bf),
            vm((3 * two, rows, latent), bf),
            vm((3 * per, groups, rows, latent), bf),
            vm((3 * per, groups, rope, rows), bf),
            vm((4, 2 * rows, span), f32),
            vm((2 * rows, 128), f32),
            vm((2 * rows, 128), f32),
            vm((2 * rows, latent), f32),
            vm((3 * per, groups, rows, latent), bf),
            vm((3 * per, groups, 8, rows), f32),
            vm((3 * two, n_ctx, rows, latent), bf),
            vm((3 * two, n_ctx, 8, rows), f32),
            vm((3 * two, rows, latent), bf),
            vm((3 * two, rows, vdim), bf),
            vm((3 * two, 8, rows), f32),
            vm((high, rows, vdim), bf),
            vm((high, 8, rows), f32),
            vm((4 * per, rows, vdim), bf),
            vm((4 * per, 8, rows), f32),
            dma((3,)),
            dma((3 * high, 2)),
            dma((3 * two, 2)),
            dma((chunks,)),
            dma((per, 4, 2)),
            dma((2 * per, 2, 2)),
            dma((3 * per * (groups - 1), 2)),
            dma((3 * per, groups, 2)),
            dma((3 * per * (groups - 1), 2)),
            dma((3 * two, n_ctx, 2)),
            dma((3 * two, 2)),
            dma((high, 2)),
            dma((4 * per, 2)),
        ],
        compiler_params=pltpu.CompilerParams(
            collective_id=0, has_side_effects=True, vmem_limit_bytes=62 * 1024 * 1024
        ),
    )(inverse, lengths, turned, qn, qr, new, w_key, value_up_weight)
    return out.reshape(own, heads, steps, vdim).swapaxes(1, 2).reshape(own, steps, heads * vdim)


def solution(mesh):
    placed = (
        P(None, ("ctx", "req"), "role"),
        P(),
        P(),
        P("req", None, ("role", "ctx")),
        P("req", None, ("role", "ctx")),
        P("req", None, None),
        P(("role", "ctx"), None, None),
        P(("role", "ctx"), None, None),
    )
    return jax.shard_map(
        shards,
        mesh=mesh,
        in_specs=placed,
        out_specs=P("req", None, ("role", "ctx")),
        check_vma=False,
    )
```

profile of v0, /device:TPU:0, one launch (start us, length us, event | category | flops | bytes accessed | tf_op | source)
XLA Modules:
  0.0 74.0 jit_solution(12203682187775987948)
XLA Ops:
  0.0 1.3 %select_reduce_fusion.inv_ref = s32[16]{0:T(128)} fusion(s32[16]{0:T(128)} %param.10), kind=kLoop, calls=%fused_computation | loop fusion | flops 752 | bytes 128 | tf_op jit(solution)/shard_map/reduce_sum | solution.py:374
  1.3 0.9 %reshape.21 = bf16[2,4,32,64]{3,2,1,0:T(8,128)(2,1)S(1)} reshape(bf16[2,4,2048]{2,1,0:T(4,128)(2,1)} %param.12) | data formatting | bytes 65536 | tf_op jit(solution)/shard_map/reshape | solution.py:379
  2.3 0.7 copy.18.qr_ref
  3.0 1.4 %pad.4.new_ref = bf16[2,128,576]{2,1,0:T(8,128)(2,1)} pad(bf16[2,4,576]{2,1,0:T(4,128)(2,1)} %param.13, bf16[]{:T(256)} %constant.3.clone.1), padding=0_0x0_124x0_0 | pad | bytes 304130 | tf_op jit(solution)/shard_map/jit(_pad)/pad | solution.py:380
  4.4 68.1 %shard_map.82 = bf16[2,128,128]{2,1,0:T(8,128)(2,1)} custom-call(s32[16]{0:T(128)} %select_reduce_fusion.inv_ref, s32[16]{0:T(128)} %len_ref.1, bf16[16,288,512]{2,1,0:T(8,128)(2,1)} %bitcast.14, bf16[2,128,128]{2,1,0:T(8,128)(2,1)} %bitcast.17, bf16[2,64,128]{2,1,0:T(8,128)(2,1)} %copy.18.qr_ref, bf16[2,128,576]{2,1,0:T(8,128)(2,1)} %pad.4.new_ref, ...), custom_call_target="tpu_custom_call" | custom-call | tf_op jit(solution)/shard_map/pallas_call | solution.py:387
  72.5 1.5 %copy.21 = bf16[2,4,4096]{2,1,0:T(4,128)(2,1)} copy(bf16[2,4,4096]{2,1,0:T(4,128)(2,1)} %bitcast.15) | data formatting | bytes 131072
  (1 shorter events, 0.0 us)
where the time goes:
time: 74.3 us; the launch traced here: 74 us
  Pallas kernels  68.1 us (92%)
  local copies, waits for them, and re-layouts  4.55 us (6%)
  other arithmetic  1.34 us (2%)
    pallas_call x1, Pallas kernels, shards(): pl.pallas_call(functools.partial(kernel, (n_req, n_ctx, steps, scale2)),...  68.1 us
    reshape x3, local copies, waits for them, and re-layouts, shards(): q_rope.reshape(own, steps, heads, rope).transpose(0, 3, 2, 1)  1.62 us
    unnamed x1, local copies, waits for them, and re-layouts  1.49 us

commit v1 on v0

v1 whole, which is shorter than its diff:
```python
import functools
import math

import jax
import jax.numpy as jnp
from jax import lax
from jax.experimental import pallas as pl
from jax.experimental.pallas import tpu as pltpu
from jax.sharding import PartitionSpec as P

NEG = -1e30
LOW = -1e29
MESH = pl.DeviceIdType.MESH
BLOCK_HEADS = 4


def xor_bit(value, bit, flip):
    b = lax.rem(lax.div(value, bit), 2)
    return value + flip * bit * (1 - 2 * b)


def owner_of(cl, k, chip):
    if cl == 0:
        return lax.rem(chip, 4) + 4 * k
    if cl == 1:
        return lax.rem(chip, 2) + 2 * lax.rem(k, 2) + 8 * lax.div(k, 2)
    return lax.rem(k, 2) + 2 * lax.rem(lax.div(chip, 2), 2) + 4 + 8 * lax.div(k, 2)


def neighbour(cl, p, chip):
    if cl == 0:
        return xor_bit(xor_bit(chip, 1, p % 2), 2, p // 2)
    return xor_bit(chip, cl, p)


def kernel(dims, slot_ref, len_ref, cache_ref, qn_ref, qr_ref, new_ref, wk_ref, vu_ref, out_ref,
           cache_v, ksend, k_a, k_b, wk_v, vu_v, qn_f, qr_f, qn_s, qr_s, new_f, rawn, rawr, qa, q_in, r_in,
           m_st, l_st, acc, o_out, e_out, o_in, e_in, merged, att_out, f_out, att_a, f_a, att_b, f_b, fin,
           load_sem, raw_ss, raw_rs, k_ss, ka_rs, kb_rs, q_ss, q_rs, o_ss, o_rs, t_ss, ta_rs, tb_rs):
    n_req, n_ctx, scale2 = dims
    role, ctx, req = lax.axis_index("role"), lax.axis_index("ctx"), lax.axis_index("req")
    per = n_req // 8
    two = 2 * per
    high = n_req // 4
    total, half, span = cache_ref.shape
    heads, nope, latent = wk_ref.shape
    own, steps = qn_ref.shape[:2]
    rows = heads * steps
    pairs = heads // 2
    low, hi = lax.rem(req, 4), lax.div(req, 4)
    bit2 = lax.rem(hi, 2)
    other = 1 - role

    def role_at(rr):
        return role if rr == 0 else other

    def ctx_at(t):
        return lax.rem(ctx + t, n_ctx)

    loads = [pltpu.make_async_copy(cache_ref, cache_v, load_sem.at[0]),
             pltpu.make_async_copy(wk_ref, wk_v, load_sem.at[1]),
             pltpu.make_async_copy(vu_ref, vu_v, load_sem.at[2])]
    loads[0].start()
    loads[1].start()

    partners = []
    for d in (1, 2, 3):
        for rr in (0, 1):
            partners.append((role_at(rr), ctx, neighbour(0, d, req)))
    for t in range(n_ctx):
        for rr in (0, 1):
            if t or rr:
                partners.append((role_at(rr), ctx_at(t), req))
    for v in range(1, high):
        far = 4 * lax.rem(hi + v, high)
        for d in (0, 1, 2):
            partners.append((role, ctx, neighbour(0, d, low) + far))
    barrier = pltpu.get_barrier_semaphore()
    for dev in partners:
        pl.semaphore_signal(barrier, inc=1, device_id=dev, device_id_type=MESH)

    started = []

    def send(src, dst, ss, rs, dev):
        copy = pltpu.make_async_remote_copy(src_ref=src, dst_ref=dst, send_sem=ss, recv_sem=rs, device_id=dev,
                                            device_id_type=MESH)
        copy.start()
        started.append(copy)

    def arrived(ref, sem):
        pltpu.make_async_copy(ref, ref, sem).wait()

    def first_row(h):
        return ((h % 2) * pairs + h // 2) * steps

    for slot in range(own):
        for h in range(heads):
            r = first_row(h)
            qn_f[slot, r:r + steps, :] = qn_ref[slot, :, h * nope:(h + 1) * nope].astype(jnp.float32)
        for h in range(pairs):
            qr_f[slot, h * steps:(h + 1) * steps, :] = qr_ref[slot, :, h * 128:(h + 1) * 128].astype(jnp.float32)
        qn_s[slot] = qn_f[slot].astype(jnp.bfloat16)
        qr_s[slot] = qr_f[slot].astype(jnp.bfloat16)
    new_f[...] = jnp.zeros_like(new_f)
    for slot in range(own):
        fresh_rows = new_ref[slot].astype(jnp.float32)
        new_f[slot, :steps, :latent] = fresh_rows[:, :latent]
        new_f[slot, :steps, latent:] = jnp.concatenate([fresh_rows[:, latent:]] * 2, axis=1)

    def request_of(slot):
        def body(j, acc_):
            return jnp.where(slot_ref[j] == slot, j, acc_)
        if total <= 16:
            r = jnp.int32(0)
            for j in range(total):
                r = body(j, r)
            return r
        return lax.fori_loop(0, total, body, jnp.int32(0))

    def k_ref(cl, m, p):
        return k_a.at[m, p] if cl == 0 else k_b.at[(cl - 1) * per + m, p]

    def k_sem(cl, m, p, h):
        return ka_rs.at[m, p, h] if cl == 0 else kb_rs.at[(cl - 1) * per + m, p, h]

    mine_rows = pl.ds(pl.multiple_of(role * half, 16), half)
    order = [(1, 1), (2, 1), (1, 0), (2, 0), (0, 1), (0, 2), (0, 3), (0, 0)]
    todo, lengths = [], {}
    for cl, p in order:
        for rr in (0, 1):
            for m in range(per):
                chip = neighbour(cl, p, req)
                slot = 2 * owner_of(cl, 2 * m + role_at(rr), chip) + (1 if cl else 0)
                todo.append((cl, p, rr, m, chip, request_of(slot)))
    loads[0].wait()
    loads[2].start()
    pending = []
    chunk = 0
    for cl, p, rr, m, chip, request in todo:
        dst = k_ref(cl, m, p)
        if p == 0 and rr == 0:
            dst[mine_rows, :] = cache_v[request]
            lengths[cl, m] = len_ref[request]
            continue
        ksend[chunk] = cache_v[request]
        pending.append((ksend.at[chunk], dst.at[mine_rows, :], k_ss.at[chunk], k_sem(cl, m, p, role),
                        (role_at(rr), ctx, chip)))
        chunk += 1

    kk = jnp.where(bit2 == 0, lax.rem(lax.div(req, 2), 2), lax.rem(req, 2)) + 2 * lax.div(req, 8)
    low_b = jnp.where(bit2 == 0, xor_bit(low, 2, 1), xor_bit(low, 1, 1))
    raws = ((1, (1 + bit2) * two + kk, [(u, v) for v in range(high) for u in (0, 1) if u or v]),
            (0, hi, [(0, v) for v in range(1, high)]))
    for slot, spot, dests in raws:
        rawn[spot] = qn_s[slot]
        rawr[spot] = qr_s[slot]

    pl.semaphore_wait(barrier, len(partners))

    index = 0
    for slot, spot, dests in raws:
        for u, v in dests:
            chip = (low_b if u else low) + 4 * lax.rem(hi + v, high)
            dev = (role, ctx, chip)
            send(qn_s.at[slot], rawn.at[spot], raw_ss.at[index, 0], raw_rs.at[spot, 0], dev)
            send(qr_s.at[slot], rawr.at[spot], raw_ss.at[index, 1], raw_rs.at[spot, 1], dev)
            index += 1
    for one in pending:
        send(*one)

    loads[1].wait()
    block = BLOCK_HEADS * steps
    half_blocks = pairs // BLOCK_HEADS
    lhs_rows = lax.broadcasted_iota(jnp.int32, (two * block, BLOCK_HEADS * nope), 0)
    lhs_cols = lax.broadcasted_iota(jnp.int32, (two * block, BLOCK_HEADS * nope), 1)
    diagonal = (lax.div(lax.rem(lhs_rows, block), steps) == lax.div(lhs_cols, nope)).astype(jnp.float32)
    diagonal = diagonal.astype(jnp.bfloat16)

    def head_at(hb, j):
        return 2 * (BLOCK_HEADS * lax.rem(hb, half_blocks) + j) + lax.div(hb, half_blocks)

    qcount = 0
    for cl in (1, 2, 0):
        for k in range(two):
            @pl.when(owner_of(cl, jnp.int32(k), req) != req)
            def _():
                arrived(rawn.at[cl * two + k], raw_rs.at[cl * two + k, 0])
                arrived(rawr.at[cl * two + k], raw_rs.at[cl * two + k, 1])

        def absorb(hb, carry):
            r0 = pl.multiple_of(hb * block, block)
            lhs = jnp.concatenate([rawn[cl * two + k, pl.ds(r0, block), :] for k in range(two)], axis=0)
            lhs = jnp.concatenate([lhs] * BLOCK_HEADS, axis=1) * diagonal
            w = jnp.concatenate([wk_v[head_at(hb, j)] for j in range(BLOCK_HEADS)], axis=0)
            res = jnp.dot(lhs, w, preferred_element_type=jnp.float32).astype(jnp.bfloat16)
            for k in range(two):
                qa[cl * two + k, pl.ds(r0, block), :] = res[k * block:(k + 1) * block]
            return carry

        lax.fori_loop(0, heads // BLOCK_HEADS, absorb, 0)
        for t in list(range(1, n_ctx)) + [0]:
            for rr in (0, 1):
                for m in range(per):
                    if t == 0 and rr == 0:
                        continue
                    k = cl * two + 2 * m + role_at(rr)
                    at = ((n_ctx - t) % n_ctx) * 2 + rr
                    dev = (role_at(rr), ctx_at(t), req)
                    send(rawr.at[k], r_in.at[cl * per + m, at], q_ss.at[qcount, 1], q_rs.at[cl * per + m, at, 1], dev)
                    send(qa.at[k], q_in.at[cl * per + m, at], q_ss.at[qcount, 0], q_rs.at[cl * per + m, at, 0], dev)
                    qcount += 1

    nt = (((1,), (1,)), ((), ()))
    rels = list(range(1, n_ctx)) + [0]
    lane = lax.broadcasted_iota(jnp.int32, (rows // 2, 128), 1)
    even = (lane < 64).astype(jnp.float32).astype(jnp.bfloat16)
    odd = (lane >= 64).astype(jnp.float32).astype(jnp.bfloat16)

    def queries(cl, m, rel):
        sl, k = cl * per + m, cl * two + 2 * m + role
        if rel == 0:
            q_own, r_own = qa[k], rawr[k]
        else:
            q_own, r_own = q_in[sl, rel * 2], r_in[sl, rel * 2]
        r_far = r_in[sl, rel * 2 + 1]
        q = jnp.concatenate([q_own, q_in[sl, rel * 2 + 1]], axis=0)
        qr = jnp.concatenate([r_own * even, r_own * odd, r_far * even, r_far * odd], axis=0)
        return q, qr

    def open_slot(cl, m):
        sl = cl * per + m
        fresh_on = jnp.logical_and(owner_of(cl, 2 * m + role, req) == req, ctx == 0)
        new = new_f[1 if cl else 0].astype(jnp.bfloat16)
        for nth, rel in enumerate(rels):
            for rr in (0, 1):
                if rel or rr:
                    arrived(q_in.at[sl, rel * 2 + rr], q_rs.at[sl, rel * 2 + rr, 0])
                    arrived(r_in.at[sl, rel * 2 + rr], q_rs.at[sl, rel * 2 + rr, 1])
            q, qr = queries(cl, m, rel)
            fresh = (lax.dot_general(q, new[:, :latent], nt, preferred_element_type=jnp.float32)
                     + lax.dot_general(qr, new[:, latent:], nt, preferred_element_type=jnp.float32)) * scale2
            token = lax.broadcasted_iota(jnp.int32, fresh.shape, 1)
            step = lax.rem(lax.broadcasted_iota(jnp.int32, fresh.shape, 0), steps)
            fresh = jnp.where(token <= jnp.where(fresh_on, step, -1), fresh, NEG)
            top = jnp.maximum(jnp.max(fresh, axis=1, keepdims=True), LOW)
            weights = jnp.exp2(fresh - top)
            m_st[nth] = jnp.broadcast_to(top, (2 * rows, 128))
            l_st[nth] = jnp.broadcast_to(jnp.sum(weights, axis=1, keepdims=True), (2 * rows, 128))
            acc[nth] = jnp.dot(weights.astype(jnp.bfloat16), new[:, :latent], preferred_element_type=jnp.float32)

    def await_part(cl, m, p):
        sample = k_ref(cl, m, 0).at[pl.ds(0, half), :]

        @pl.when(p > 0)
        def _():
            arrived(sample, k_sem(cl, m, p, role))
        arrived(sample, k_sem(cl, m, p, other))

    def part(cl, m, p, nth):
        q, qr = queries(cl, m, rels[nth])
        keys = k_ref(cl, m, p)
        rotary = keys[latent:, :]
        s = jnp.dot(q, keys[:latent, :], preferred_element_type=jnp.float32)
        s += jnp.dot(qr, jnp.concatenate([rotary, rotary], axis=0), preferred_element_type=jnp.float32)
        if cl == 0:
            chip = xor_bit(xor_bit(req, 1, lax.rem(p, 2)), 2, lax.div(p, 2))
        else:
            chip = xor_bit(req, cl, p)
        position = (ctx * n_req + chip) * span + lax.broadcasted_iota(jnp.int32, (1, span), 1)
        s = jnp.where(position < lengths[cl, m], s * scale2, NEG)
        before = m_st[nth][:, :1]
        top = jnp.maximum(before, jnp.max(s, axis=1, keepdims=True))
        keep = jnp.exp2(before - top)
        w = jnp.exp2(s - top)
        m_st[nth] = jnp.broadcast_to(top, (2 * rows, 128))
        l_st[nth] = l_st[nth] * keep + jnp.sum(w, axis=1, keepdims=True)
        acc[nth] = acc[nth] * keep + lax.dot_general(w.astype(jnp.bfloat16), keys[:latent, :], nt,
                                                     preferred_element_type=jnp.float32)

    ocount = [0]

    def close_block(cl, m, nth):
        rel = rels[nth]
        sl, k = cl * per + m, cl * two + 2 * m + role
        back = (n_ctx - rel) % n_ctx
        norm = l_st[nth][:, :1]
        live = norm > 0.0
        safe = jnp.where(live, norm, 1.0)
        o = (acc[nth] * (1.0 / safe)).astype(jnp.bfloat16)
        norm = l_st[nth]
        lse = jnp.where(norm > 0.0, m_st[nth] + jnp.log2(jnp.where(norm > 0.0, norm, 1.0)), NEG)
        for rr in (0, 1):
            piece = o[rr * rows:(rr + 1) * rows]
            e = lse[rr * rows:(rr + 1) * rows].T[:8]
            if rel == 0 and rr == 0:
                o_in[k, 0] = piece
                e_in[k, 0] = e
                continue
            o_out[sl, rel * 2 + rr] = piece
            e_out[sl, rel * 2 + rr] = e
        for rr in (0, 1):
            if rel == 0 and rr == 0:
                continue
            dev = (role_at(rr), ctx_at(rel), req)
            n = ocount[0]
            send(e_out.at[sl, rel * 2 + rr], e_in.at[k, back], o_ss.at[n, 1], o_rs.at[k, back, 1], dev)
            send(o_out.at[sl, rel * 2 + rr], o_in.at[k, back], o_ss.at[n, 0], o_rs.at[k, back, 0], dev)
            ocount[0] += 1

    def parts_of(cl, m, first, last):
        def body(p, carry):
            await_part(cl, m, p)
            for nth in range(n_ctx):
                part(cl, m, p, nth)
            return carry
        lax.fori_loop(first, last, body, 0)

    def last_part(cl, m, p):
        p = jnp.int32(p)
        await_part(cl, m, p)
        for nth in range(n_ctx):
            part(cl, m, p, nth)
            close_block(cl, m, nth)

    out_rows = lax.broadcasted_iota(jnp.int32, (two * block, 128), 0)
    which = lax.div(lax.rem(out_rows, block), steps)
    guarded = []

    def spread(row):
        return jnp.broadcast_to(row[:1], (128, rows)).T

    def merge(cl):
        for rr in (0, 1):
            for m in range(per):
                k = cl * two + 2 * m + role_at(rr)
                for rel in range(n_ctx):
                    if rr or rel:
                        arrived(o_in.at[k, rel], o_rs.at[k, rel, 0])
                        arrived(e_in.at[k, rel], o_rs.at[k, rel, 1])
                es = [e_in[k, rel] for rel in range(n_ctx)]
                top = functools.reduce(jnp.maximum, es)
                shares = [jnp.exp2(e - top) for e in es]
                norm = sum(shares)
                f_out[k] = top + jnp.log2(norm)
                value = 0.0
                for rel in range(n_ctx):
                    w = jnp.concatenate([spread(shares[rel] / norm)] * (latent // 128), axis=1)
                    value = value + o_in[k, rel].astype(jnp.float32) * w
                merged[k] = value.astype(jnp.bfloat16)

        def up(hb, carry):
            r0 = pl.multiple_of(hb * block, block)
            lhs = jnp.concatenate([merged[cl * two + k, pl.ds(r0, block), :] for k in range(two)], axis=0)
            res = jnp.zeros((two * block, 128), jnp.float32)
            for j in range(BLOCK_HEADS):
                one = jnp.dot(lhs, vu_v[head_at(hb, j)], preferred_element_type=jnp.float32)
                res = jnp.where(which == j, one, res)
            res = res.astype(jnp.bfloat16)
            for k in range(two):
                att_out[cl * two + k, pl.ds(r0, block), :] = res[k * block:(k + 1) * block]
            return carry

        lax.fori_loop(0, heads // BLOCK_HEADS, up, 0)
        for k in range(two):
            e = cl * two + k
            owner = owner_of(cl, jnp.int32(k), req)
            if cl == 0:
                at, dst, fdst, sems = hi, att_a, f_a, ta_rs
            elif cl == 1:
                at, dst, fdst, sems = lax.div(req, 2), att_b, f_b, tb_rs
            else:
                at, dst, fdst, sems = lax.rem(req, 2) + 2 * hi, att_b, f_b, tb_rs
            copies = [
                pltpu.make_async_remote_copy(
                    src_ref=src.at[e], dst_ref=d.at[at], send_sem=t_ss.at[e, j], recv_sem=sems.at[at, j],
                    device_id=(role, ctx, owner), device_id_type=MESH)
                for j, (src, d) in enumerate(((att_out, dst), (f_out, fdst)))
            ]

            @pl.when(owner != req)
            def _():
                for copy in copies:
                    copy.start()

            @pl.when(owner == req)
            def _():
                dst[at] = att_out[e]
                fdst[at] = f_out[e]
            guarded.append((owner, copies))

    own_b = jnp.where(bit2 == 0, lax.div(req, 2), lax.rem(req, 2) + 2 * hi)

    def combine(slot):
        count, src, fsrc, sems, mine = ((high, att_a, f_a, ta_rs, hi), (4 * per, att_b, f_b, tb_rs, own_b))[slot]
        for j in range(count):
            @pl.when(mine != j)
            def _():
                arrived(src.at[j], sems.at[j, 0])
                arrived(fsrc.at[j], sems.at[j, 1])
        es = [fsrc[j] for j in range(count)]
        top = functools.reduce(jnp.maximum, es)
        shares = [jnp.exp2(e - top) for e in es]
        norm = sum(shares)
        value = 0.0
        for j in range(count):
            value = value + src[j].astype(jnp.float32) * spread(shares[j] / norm)
        fin[slot] = value
        for h in range(heads):
            r = first_row(h)
            out_ref[slot, :, h * 128:(h + 1) * 128] = fin[slot, r:r + steps, :].astype(jnp.bfloat16)

    for cl in (1, 2):
        for m in range(per):
            open_slot(cl, m)
            parts_of(cl, m, 0, 1)
            last_part(cl, m, 1)
    for m in range(per):
        open_slot(0, m)
        parts_of(0, m, 0, 3)
        if m == per - 1:
            loads[2].wait()
            merge(1)
            merge(2)
        last_part(0, m, 3)
    combine(1)
    merge(0)
    combine(0)

    for copy in started:
        copy.wait_send()
    for owner, copies in guarded:
        @pl.when(owner != req)
        def _():
            for copy in copies:
                copy.wait_send()


def shards(cache, lengths, request_decode_slot, q_nope, q_rope, new_latent, w_key, value_up_weight):
    total = request_decode_slot.shape[0]
    n_req, n_ctx = lax.axis_size("req"), lax.axis_size("ctx")
    heads, nope, latent = w_key.shape
    vdim = value_up_weight.shape[2]
    own, steps = q_nope.shape[:2]
    rope = q_rope.shape[2] // heads
    span, half = cache.shape[1:]
    rows = heads * steps
    per, two, high = n_req // 8, n_req // 4, n_req // 4
    groups = 2 * n_ctx
    scale2 = (nope + rope) ** (-0.5) * math.log2(math.e)

    turned = jnp.swapaxes(cache, 1, 2)
    bf, f32 = jnp.bfloat16, jnp.float32
    chunks = total - 3 * per
    vm, dma = pltpu.VMEM, pltpu.SemaphoreType.DMA
    smem = pl.BlockSpec(memory_space=pltpu.SMEM)
    here = pl.BlockSpec(memory_space=pltpu.VMEM)
    away = pl.BlockSpec(memory_space=pl.ANY)
    return pl.pallas_call(
        functools.partial(kernel, (n_req, n_ctx, scale2)),
        out_shape=jax.ShapeDtypeStruct((own, steps, heads * vdim), bf),
        in_specs=[smem, smem, away, here, here, here, away, away],
        out_specs=here,
        scratch_shapes=[
            vm((total, half, span), bf),
            vm((chunks, half, span), bf),
            vm((per, 4, 2 * half, span), bf),
            vm((2 * per, 2, 2 * half, span), bf),
            vm(w_key.shape, bf),
            vm(value_up_weight.shape, bf),
            vm((own, rows, nope), f32),
            vm((own, rows // 2, 2 * rope), f32),
            vm((own, rows, nope), bf),
            vm((own, rows // 2, 2 * rope), bf),
            vm((own, 128, latent + 2 * rope), f32),
            vm((3 * two, rows, nope), bf),
            vm((3 * two, rows // 2, 2 * rope), bf),
            vm((3 * two, rows, latent), bf),
            vm((3 * per, groups, rows, latent), bf),
            vm((3 * per, groups, rows // 2, 2 * rope), bf),
            vm((n_ctx, 2 * rows, 128), f32),
            vm((n_ctx, 2 * rows, 128), f32),
            vm((n_ctx, 2 * rows, latent), f32),
            vm((3 * per, groups, rows, latent), bf),
            vm((3 * per, groups, 8, rows), f32),
            vm((3 * two, n_ctx, rows, latent), bf),
            vm((3 * two, n_ctx, 8, rows), f32),
            vm((3 * two, rows, latent), bf),
            vm((3 * two, rows, vdim), bf),
            vm((3 * two, 8, rows), f32),
            vm((high, rows, vdim), bf),
            vm((high, 8, rows), f32),
            vm((4 * per, rows, vdim), bf),
            vm((4 * per, 8, rows), f32),
            vm((own, rows, vdim), f32),
            dma((3,)),
            dma((3 * high, 2)),
            dma((3 * two, 2)),
            dma((chunks,)),
            dma((per, 4, 2)),
            dma((2 * per, 2, 2)),
            dma((3 * per * (groups - 1), 2)),
            dma((3 * per, groups, 2)),
            dma((3 * per * (groups - 1), 2)),
            dma((3 * two, n_ctx, 2)),
            dma((3 * two, 2)),
            dma((high, 2)),
            dma((4 * per, 2)),
        ],
        compiler_params=pltpu.CompilerParams(
            collective_id=0, has_side_effects=True, vmem_limit_bytes=62 * 1024 * 1024
        ),
    )(request_decode_slot, lengths, turned, q_nope, q_rope, new_latent, w_key, value_up_weight)


def solution(mesh):
    placed = (
        P(None, ("ctx", "req"), "role"),
        P(),
        P(),
        P("req", None, ("role", "ctx")),
        P("req", None, ("role", "ctx")),
        P("req", None, None),
        P(("role", "ctx"), None, None),
        P(("role", "ctx"), None, None),
    )
    return jax.shard_map(
        shards,
        mesh=mesh,
        in_specs=placed,
        out_specs=P("req", None, ("role", "ctx")),
        check_vma=False,
    )
```

time: 74.3 us -> 68.6 us (0.923)
  local copies, waits for them, and re-layouts: 4.55 us -> 1.49 us
  other arithmetic: 1.34 us -> 0 us
  Pallas kernels: 68.1 us -> 66.9 us
    reshape x3 -> x0, local copies, waits for them, and re-layouts: 1.62 us -> none  [shards(): q_rope.reshape(own, steps, heads, rope).transpose(0, 3, 2, 1)]
    pad x1 -> x0, local copies, waits for them, and re-layouts: 1.44 us -> none  [shards(): new = jnp.pad(new_latent, ((0, 0), (0, 128 - steps), (0, 0)))]
    reduce_sum x1 -> x0, other arithmetic: 1.34 us -> none  [shards(): jnp.sum(jnp.where(request_decode_slot[None, :] == slots[:, None], slots[N...]
    pallas_call x1, Pallas kernels: 68.1 us -> 66.9 us  [shards(): pl.pallas_call(functools.partial(kernel, (n_req, n_ctx, scale2)), out_sha...]
where the time goes in v1:
time: 68.6 us; the launch traced here: 68.4 us
  Pallas kernels  66.9 us (98%)
  local copies, waits for them, and re-layouts  1.49 us (2%)
    pallas_call x1, Pallas kernels, shards(): pl.pallas_call(functools.partial(kernel, (n_req, n_ctx, scale2)), out_sha...  66.9 us
    unnamed x1, local copies, waits for them, and re-layouts  1.49 us

profile of v1, /device:TPU:0, one launch (start us, length us, event | category | flops | bytes accessed | tf_op | source)
XLA Modules:
  0.0 68.4 jit_solution(7833331951502719075)
XLA Ops:
  0.0 66.9 %shard_map.82 = bf16[2,4,4096]{2,1,0:T(4,128)(2,1)} custom-call(s32[16]{0:T(128)} %slot_ref.1, s32[16]{0:T(128)} %len_ref.1, bf16[16,288,512]{2,1,0:T(8,128)(2,1)} %bitcast.1, bf16[2,4,4096]{2,1,0:T(4,128)(2,1)} %qn_ref.1, bf16[2,4,2048]{2,1,0:T(4,128)(2,1)} %qr_ref.1, bf16[2,4,576]{2,1,0:T(4,128)(2,1)} %new_ref.1, bf16[32,128,512]{2,1,0:T(8,128)(2,1)} %wk_ref.1, ...), custom_call_target="tpu_custom_call" | custom-call | tf_op jit(solution)/shard_map/pallas_call | solution.py:458
  66.9 1.5 %copy.10 = bf16[2,4,4096]{2,1,0:T(4,128)(2,1)} copy(bf16[2,4,4096]{2,1,0:T(4,128)(2,1)} %shard_map.82) | data formatting | bytes 131072

commit v2 on v1

--- a/solution.py
+++ b/solution.py
@@ -12,6 +12,7 @@
 LOW = -1e29
 MESH = pl.DeviceIdType.MESH
 BLOCK_HEADS = 4
+UNROLL = 4
 
 
 def xor_bit(value, bit, flip):
@@ -33,10 +34,10 @@
     return xor_bit(chip, cl, p)
 
 
-def kernel(dims, slot_ref, len_ref, cache_ref, qn_ref, qr_ref, new_ref, wk_ref, vu_ref, out_ref,
-           cache_v, ksend, k_a, k_b, wk_v, vu_v, qn_f, qr_f, qn_s, qr_s, new_f, rawn, rawr, qa, q_in, r_in,
+def kernel(dims, slot_ref, len_ref, cache_ref, qn_any, qr_any, new_any, wk_ref, vu_ref, out_ref,
+           qn_ref, qr_ref, new_ref, cache_v, ksend, k_a, k_b, wk_v, vu_v, qn_f, qr_f, qn_s, qr_s, new_f, rawn, rawr, qa, q_in, r_in,
            m_st, l_st, acc, o_out, e_out, o_in, e_in, merged, att_out, f_out, att_a, f_a, att_b, f_b, fin,
-           load_sem, raw_ss, raw_rs, k_ss, ka_rs, kb_rs, q_ss, q_rs, o_ss, o_rs, t_ss, ta_rs, tb_rs):
+           load_sem, cache_sem, raw_ss, raw_rs, k_ss, ka_rs, kb_rs, q_ss, q_rs, o_ss, o_rs, t_ss, ta_rs, tb_rs):
     n_req, n_ctx, scale2 = dims
     role, ctx, req = lax.axis_index("role"), lax.axis_index("ctx"), lax.axis_index("req")
     per = n_req // 8
@@ -44,7 +45,7 @@
     high = n_req // 4
     total, half, span = cache_ref.shape
     heads, nope, latent = wk_ref.shape
-    own, steps = qn_ref.shape[:2]
+    own, steps = qn_any.shape[:2]
     rows = heads * steps
     pairs = heads // 2
     low, hi = lax.rem(req, 4), lax.div(req, 4)
@@ -57,11 +58,17 @@
     def ctx_at(t):
         return lax.rem(ctx + t, n_ctx)
 
-    loads = [pltpu.make_async_copy(cache_ref, cache_v, load_sem.at[0]),
+    caches = [pltpu.make_async_copy(cache_ref.at[r], cache_v.at[r], cache_sem.at[r]) for r in range(total)]
+    loads = [None,
              pltpu.make_async_copy(wk_ref, wk_v, load_sem.at[1]),
-             pltpu.make_async_copy(vu_ref, vu_v, load_sem.at[2])]
-    loads[0].start()
-    loads[1].start()
+             pltpu.make_async_copy(vu_ref, vu_v, load_sem.at[2]),
+             pltpu.make_async_copy(qn_any, qn_ref, load_sem.at[3]),
+             pltpu.make_async_copy(qr_any, qr_ref, load_sem.at[4]),
+             pltpu.make_async_copy(new_any, new_ref, load_sem.at[5])]
+    for one in (3, 4, 5):
+        loads[one].start()
+    for copy in caches:
+        copy.start()
 
     partners = []
     for d in (1, 2, 3):
@@ -93,6 +100,8 @@
     def first_row(h):
         return ((h % 2) * pairs + h // 2) * steps
 
+    for one in (3, 4, 5):
+        loads[one].wait()
     for slot in range(own):
         for h in range(heads):
             r = first_row(h)
@@ -124,91 +133,154 @@
         return ka_rs.at[m, p, h] if cl == 0 else kb_rs.at[(cl - 1) * per + m, p, h]
 
     mine_rows = pl.ds(pl.multiple_of(role * half, 16), half)
-    order = [(1, 1), (2, 1), (1, 0), (2, 0), (0, 1), (0, 2), (0, 3), (0, 0)]
+    order = [(1, 1), (2, 1), (0, 1), (0, 2), (0, 3), (1, 0), (2, 0), (0, 0)]
     todo, lengths = [], {}
     for cl, p in order:
-        for rr in (0, 1):
+        for to in ((0, 1) if p else (role, other)):
             for m in range(per):
                 chip = neighbour(cl, p, req)
-                slot = 2 * owner_of(cl, 2 * m + role_at(rr), chip) + (1 if cl else 0)
-                todo.append((cl, p, rr, m, chip, request_of(slot)))
-    loads[0].wait()
+                slot = 2 * owner_of(cl, 2 * m + to, chip) + (1 if cl else 0)
+                todo.append((cl, p, to, m, chip, request_of(slot)))
+    for copy in caches:
+        copy.wait()
+    loads[1].start()
     loads[2].start()
-    pending = []
+    pending, delayed = [], []
     chunk = 0
-    for cl, p, rr, m, chip, request in todo:
+    for cl, p, to, m, chip, request in todo:
         dst = k_ref(cl, m, p)
-        if p == 0 and rr == 0:
+        if to is role:
             dst[mine_rows, :] = cache_v[request]
             lengths[cl, m] = len_ref[request]
             continue
         ksend[chunk] = cache_v[request]
-        pending.append((ksend.at[chunk], dst.at[mine_rows, :], k_ss.at[chunk], k_sem(cl, m, p, role),
-                        (role_at(rr), ctx, chip)))
+        first = m == 0 and cl > 0 and p > 0
+        split = first and p > 0 and to == 1
+        cut = half // 32 * 16 if split else half
+        for begin, end, early in ((0, cut, first), (cut, half, False)):
+            if begin < end:
+                rows_to = pl.ds(pl.multiple_of(role * half + begin, 16), end - begin)
+                (pending if early else delayed).append(
+                    (ksend.at[chunk, pl.ds(begin, end - begin)], dst.at[rows_to, :],
+                     k_ss.at[chunk, 0 if early else 1], k_sem(cl, m, p, role), (to, ctx, chip)))
         chunk += 1
 
     kk = jnp.where(bit2 == 0, lax.rem(lax.div(req, 2), 2), lax.rem(req, 2)) + 2 * lax.div(req, 8)
-    low_b = jnp.where(bit2 == 0, xor_bit(low, 2, 1), xor_bit(low, 1, 1))
-    raws = ((1, (1 + bit2) * two + kk, [(u, v) for v in range(high) for u in (0, 1) if u or v]),
-            (0, hi, [(0, v) for v in range(1, high)]))
-    for slot, spot, dests in raws:
-        rawn[spot] = qn_s[slot]
-        rawr[spot] = qr_s[slot]
+    mine_a, mine_b = (0, hi), (1 + bit2, kk)
+    for slot, (cl, k) in ((0, mine_a), (1, mine_b)):
+        rawn[cl * two + k] = qn_s[slot]
+        rawr[cl * two + k] = qr_s[slot]
 
     pl.semaphore_wait(barrier, len(partners))
 
-    index = 0
-    for slot, spot, dests in raws:
-        for u, v in dests:
-            chip = (low_b if u else low) + 4 * lax.rem(hi + v, high)
-            dev = (role, ctx, chip)
-            send(qn_s.at[slot], rawn.at[spot], raw_ss.at[index, 0], raw_rs.at[spot, 0], dev)
-            send(qr_s.at[slot], rawr.at[spot], raw_ss.at[index, 1], raw_rs.at[spot, 1], dev)
-            index += 1
+    rcount = [0]
+
+    def share_raw(n_src, r_src, spot, dev):
+        n = rcount[0]
+        send(n_src, rawn.at[spot], raw_ss.at[n, 0], raw_rs.at[spot, 0], dev)
+        send(r_src, rawr.at[spot], raw_ss.at[n, 1], raw_rs.at[spot, 1], dev)
+        rcount[0] += 1
+
+    def flipped(chip, bit):
+        return jnp.where(bit == 0, xor_bit(chip, 2, 1), xor_bit(chip, 1, 1))
+
+    spot_a, spot_b = hi, (1 + bit2) * two + kk
+    for v in range(1, high):
+        chip = low + 4 * lax.rem(hi + v, high)
+        share_raw(qn_s.at[1], qr_s.at[1], spot_b, (role, ctx, chip))
+        share_raw(qn_s.at[0], qr_s.at[0], spot_a, (role, ctx, chip))
+    share_raw(qn_s.at[1], qr_s.at[1], spot_b, (role, ctx, flipped(req, bit2)))
     for one in pending:
         send(*one)
 
-    loads[1].wait()
     block = BLOCK_HEADS * steps
     half_blocks = pairs // BLOCK_HEADS
-    lhs_rows = lax.broadcasted_iota(jnp.int32, (two * block, BLOCK_HEADS * nope), 0)
-    lhs_cols = lax.broadcasted_iota(jnp.int32, (two * block, BLOCK_HEADS * nope), 1)
-    diagonal = (lax.div(lax.rem(lhs_rows, block), steps) == lax.div(lhs_cols, nope)).astype(jnp.float32)
-    diagonal = diagonal.astype(jnp.bfloat16)
 
     def head_at(hb, j):
         return 2 * (BLOCK_HEADS * lax.rem(hb, half_blocks) + j) + lax.div(hb, half_blocks)
 
-    qcount = 0
-    for cl in (1, 2, 0):
-        for k in range(two):
-            @pl.when(owner_of(cl, jnp.int32(k), req) != req)
-            def _():
-                arrived(rawn.at[cl * two + k], raw_rs.at[cl * two + k, 0])
-                arrived(rawr.at[cl * two + k], raw_rs.at[cl * two + k, 1])
-
-        def absorb(hb, carry):
+    def absorb(batch):
+        shape = (len(batch) * block, BLOCK_HEADS * nope)
+        of_row = lax.div(lax.rem(lax.broadcasted_iota(jnp.int32, shape, 0), block), steps)
+        of_col = lax.div(lax.broadcasted_iota(jnp.int32, shape, 1), nope)
+        diagonal = (of_row == of_col).astype(jnp.float32).astype(jnp.bfloat16)
+
+        def body(hb, carry):
             r0 = pl.multiple_of(hb * block, block)
-            lhs = jnp.concatenate([rawn[cl * two + k, pl.ds(r0, block), :] for k in range(two)], axis=0)
+            lhs = jnp.concatenate([rawn[cl * two + k, pl.ds(r0, block), :] for cl, k in batch], axis=0)
             lhs = jnp.concatenate([lhs] * BLOCK_HEADS, axis=1) * diagonal
             w = jnp.concatenate([wk_v[head_at(hb, j)] for j in range(BLOCK_HEADS)], axis=0)
             res = jnp.dot(lhs, w, preferred_element_type=jnp.float32).astype(jnp.bfloat16)
-            for k in range(two):
-                qa[cl * two + k, pl.ds(r0, block), :] = res[k * block:(k + 1) * block]
+            for n, (cl, k) in enumerate(batch):
+                qa[cl * two + k, pl.ds(r0, block), :] = res[n * block:(n + 1) * block]
             return carry
 
-        lax.fori_loop(0, heads // BLOCK_HEADS, absorb, 0)
-        for t in list(range(1, n_ctx)) + [0]:
-            for rr in (0, 1):
-                for m in range(per):
-                    if t == 0 and rr == 0:
-                        continue
-                    k = cl * two + 2 * m + role_at(rr)
-                    at = ((n_ctx - t) % n_ctx) * 2 + rr
-                    dev = (role_at(rr), ctx_at(t), req)
-                    send(rawr.at[k], r_in.at[cl * per + m, at], q_ss.at[qcount, 1], q_rs.at[cl * per + m, at, 1], dev)
-                    send(qa.at[k], q_in.at[cl * per + m, at], q_ss.at[qcount, 0], q_rs.at[cl * per + m, at, 0], dev)
-                    qcount += 1
+        lax.fori_loop(0, heads // BLOCK_HEADS, body, 0, unroll=UNROLL)
+
+    guarded = []
+    qcount = [0]
+
+    def share_queries(batch):
+        for cl, k in batch:
+            e, to = cl * two + k, lax.rem(k, 2)
+            sl, rr = cl * per + lax.div(k, 2), lax.rem(to + role, 2)
+            for t in list(range(1, n_ctx)) + [0]:
+                at = ((n_ctx - t) % n_ctx) * 2 + rr
+                n = qcount[0]
+                copies = [
+                    pltpu.make_async_remote_copy(
+                        src_ref=src.at[e], dst_ref=dst.at[sl, at], send_sem=q_ss.at[n, j], recv_sem=q_rs.at[sl, at, j],
+                        device_id=(to, ctx_at(t), req), device_id_type=MESH)
+                    for j, (src, dst) in ((1, (rawr, r_in)), (0, (qa, q_in)))
+                ]
+                if t:
+                    for copy in copies:
+                        copy.start()
+                    started.extend(copies)
+                else:
+                    away = to != role
+
+                    @pl.when(away)
+                    def _():
+                        for copy in copies:
+                            copy.start()
+                    guarded.append((away, copies))
+                qcount[0] += 1
+
+    def raw_arrived(cl, k):
+        arrived(rawn.at[cl * two + k], raw_rs.at[cl * two + k, 0])
+        arrived(rawr.at[cl * two + k], raw_rs.at[cl * two + k, 1])
+
+    def class_b(owner):
+        bit = lax.rem(lax.div(owner, 4), 2)
+        place = jnp.where(bit == 0, lax.rem(lax.div(owner, 2), 2), lax.rem(owner, 2))
+        return bit, (1 + bit, place + 2 * lax.div(owner, 8))
+
+    loads[1].wait()
+    absorb([mine_b, mine_a])
+    share_queries([mine_b, mine_a])
+    near, far = [class_b(flipped(req, bit2))[1]], []
+    for v in range(1, high):
+        owner = low + 4 * lax.rem(hi + v, high)
+        bit, entry = class_b(owner)
+        raw_arrived(*entry)
+        spot = entry[0] * two + entry[1]
+        share_raw(rawn.at[spot], rawr.at[spot], spot, (role, ctx, flipped(req, bit)))
+        near.append(entry)
+        far.append(class_b(flipped(owner, bit))[1])
+    for one in delayed:
+        send(*one)
+    for v in range(1, high):
+        entry = (0, lax.rem(hi + v, high))
+        raw_arrived(*entry)
+        near.append(entry)
+    raw_arrived(*near[0])
+    absorb(near)
+    share_queries(near)
+    for entry in far:
+        raw_arrived(*entry)
+    absorb(far)
+    share_queries(far)
 
     nt = (((1,), (1,)), ((), ()))
     rels = list(range(1, n_ctx)) + [0]
@@ -324,8 +396,6 @@
 
     out_rows = lax.broadcasted_iota(jnp.int32, (two * block, 128), 0)
     which = lax.div(lax.rem(out_rows, block), steps)
-    guarded = []
-
     def spread(row):
         return jnp.broadcast_to(row[:1], (128, rows)).T
 
@@ -360,7 +430,7 @@
                 att_out[cl * two + k, pl.ds(r0, block), :] = res[k * block:(k + 1) * block]
             return carry
 
-        lax.fori_loop(0, heads // BLOCK_HEADS, up, 0)
+        lax.fori_loop(0, heads // BLOCK_HEADS, up, 0, unroll=UNROLL)
         for k in range(two):
             e = cl * two + k
             owner = owner_of(cl, jnp.int32(k), req)
@@ -386,7 +456,7 @@
             def _():
                 dst[at] = att_out[e]
                 fdst[at] = f_out[e]
-            guarded.append((owner, copies))
+            guarded.append((owner != req, copies))
 
     own_b = jnp.where(bit2 == 0, lax.div(req, 2), lax.rem(req, 2) + 2 * hi)
 
@@ -428,8 +498,8 @@
 
     for copy in started:
         copy.wait_send()
-    for owner, copies in guarded:
-        @pl.when(owner != req)
+    for sent, copies in guarded:
+        @pl.when(sent)
         def _():
             for copy in copies:
                 copy.wait_send()
@@ -453,14 +523,16 @@
     chunks = total - 3 * per
     vm, dma = pltpu.VMEM, pltpu.SemaphoreType.DMA
     smem = pl.BlockSpec(memory_space=pltpu.SMEM)
-    here = pl.BlockSpec(memory_space=pltpu.VMEM)
     away = pl.BlockSpec(memory_space=pl.ANY)
-    return pl.pallas_call(
+    out = pl.pallas_call(
         functools.partial(kernel, (n_req, n_ctx, scale2)),
-        out_shape=jax.ShapeDtypeStruct((own, steps, heads * vdim), bf),
-        in_specs=[smem, smem, away, here, here, here, away, away],
-        out_specs=here,
+        out_shape=pltpu.VMEM((own, steps, heads * vdim), bf),
+        in_specs=[smem, smem, away, away, away, away, away, away],
+        out_specs=pl.BlockSpec(memory_space=pltpu.VMEM),
         scratch_shapes=[
+            vm(q_nope.shape, bf),
+            vm(q_rope.shape, bf),
+            vm(new_latent.shape, bf),
             vm((total, half, span), bf),
             vm((chunks, half, span), bf),
             vm((per, 4, 2 * half, span), bf),
@@ -492,13 +564,14 @@
             vm((4 * per, rows, vdim), bf),
             vm((4 * per, 8, rows), f32),
             vm((own, rows, vdim), f32),
-            dma((3,)),
+            dma((6 + own,)),
+            dma((total,)),
             dma((3 * high, 2)),
             dma((3 * two, 2)),
-            dma((chunks,)),
+            dma((chunks, 2)),
             dma((per, 4, 2)),
             dma((2 * per, 2, 2)),
-            dma((3 * per * (groups - 1), 2)),
+            dma((3 * two * n_ctx, 2)),
             dma((3 * per, groups, 2)),
             dma((3 * per * (groups - 1), 2)),
             dma((3 * two, n_ctx, 2)),
@@ -510,6 +583,7 @@
             collective_id=0, has_side_effects=True, vmem_limit_bytes=62 * 1024 * 1024
         ),
     )(request_decode_slot, lengths, turned, q_nope, q_rope, new_latent, w_key, value_up_weight)
+    return out
 
 
 def solution(mesh):

time: 68.6 us -> 64.2 us (0.936)
  Pallas kernels: 66.9 us -> 63.4 us
  local copies, waits for them, and re-layouts: 1.49 us -> 0.63 us
    pallas_call x1, Pallas kernels: 66.9 us -> 63.4 us  [shards(): pl.pallas_call(functools.partial(kernel, (n_req, n_ctx, scale2)), out_sha...]
    unnamed x1, local copies, waits for them, and re-layouts: 1.49 us -> 0.63 us
where the time goes in v2:
time: 64.2 us; the launch traced here: 64.1 us
  Pallas kernels  63.4 us (99%)
    pallas_call x1, Pallas kernels, shards(): pl.pallas_call(functools.partial(kernel, (n_req, n_ctx, scale2)), out_sha...  63.4 us

profile of v2, /device:TPU:0, one launch (start us, length us, event | category | flops | bytes accessed | tf_op | source)
XLA Modules:
  0.0 64.1 jit_solution(17497651182491931791)
XLA Ops:
  0.0 63.4 %shard_map.82 = bf16[2,4,4096]{2,1,0:T(4,128)(2,1)S(1)} custom-call(s32[16]{0:T(128)} %slot_ref.1, s32[16]{0:T(128)} %len_ref.1, bf16[16,288,512]{2,1,0:T(8,128)(2,1)} %bitcast.1, bf16[2,4,4096]{2,1,0:T(4,128)(2,1)} %qn_any.1, bf16[2,4,2048]{2,1,0:T(4,128)(2,1)} %qr_any.1, bf16[2,4,576]{2,1,0:T(4,128)(2,1)} %new_any.1, bf16[32,128,512]{2,1,0:T(8,128)(2,1)} %wk_ref.1, ...), custom_call_target="tpu_custom_call" | custom-call | tf_op jit(solution)/shard_map/pallas_call | solution.py:527
  63.4 0.6 copy.10

commit v3 on v2

--- a/solution.py
+++ b/solution.py
@@ -12,7 +12,7 @@
 LOW = -1e29
 MESH = pl.DeviceIdType.MESH
 BLOCK_HEADS = 4
-UNROLL = 4
+UNROLL = 8
 
 
 def xor_bit(value, bit, flip):
@@ -146,6 +146,8 @@
     loads[1].start()
     loads[2].start()
     pending, delayed = [], []
+    cuts = 2 if span % 256 == 0 else 1
+    width = span // cuts
     chunk = 0
     for cl, p, to, m, chip, request in todo:
         dst = k_ref(cl, m, p)
@@ -157,6 +159,13 @@
         first = m == 0 and cl > 0 and p > 0
         split = first and p > 0 and to == 1
         cut = half // 32 * 16 if split else half
+        if cl == 0 and p == 3:
+            for c in range(cuts):
+                cols = pl.ds(c * width, width)
+                delayed.append((ksend.at[chunk, :, cols], dst.at[mine_rows, cols], k_ss.at[chunk, c],
+                                k_sem(cl, m, p + c, role), (to, ctx, chip)))
+            chunk += 1
+            continue
         for begin, end, early in ((0, cut, first), (cut, half, False)):
             if begin < end:
                 rows_to = pl.ds(pl.multiple_of(role * half + begin, 16), end - begin)
@@ -215,7 +224,7 @@
                 qa[cl * two + k, pl.ds(r0, block), :] = res[n * block:(n + 1) * block]
             return carry
 
-        lax.fori_loop(0, heads // BLOCK_HEADS, body, 0, unroll=UNROLL)
+        lax.fori_loop(0, heads // BLOCK_HEADS, body, 0, unroll=min(UNROLL, heads // BLOCK_HEADS))
 
     guarded = []
     qcount = [0]
@@ -328,49 +337,51 @@
             arrived(sample, k_sem(cl, m, p, role))
         arrived(sample, k_sem(cl, m, p, other))
 
-    def part(cl, m, p, nth):
+    def part(cl, m, p, nth, begin=0, end=2, col=0, wide=None):
+        wide = wide or span
+        at = slice(begin * rows, end * rows)
         q, qr = queries(cl, m, rels[nth])
+        q, qr = q[at], qr[at]
         keys = k_ref(cl, m, p)
-        rotary = keys[latent:, :]
-        s = jnp.dot(q, keys[:latent, :], preferred_element_type=jnp.float32)
+        columns = pl.ds(col, wide)
+        rotary = keys[latent:, columns]
+        s = jnp.dot(q, keys[:latent, columns], preferred_element_type=jnp.float32)
         s += jnp.dot(qr, jnp.concatenate([rotary, rotary], axis=0), preferred_element_type=jnp.float32)
         if cl == 0:
             chip = xor_bit(xor_bit(req, 1, lax.rem(p, 2)), 2, lax.div(p, 2))
         else:
             chip = xor_bit(req, cl, p)
-        position = (ctx * n_req + chip) * span + lax.broadcasted_iota(jnp.int32, (1, span), 1)
+        position = (ctx * n_req + chip) * span + col + lax.broadcasted_iota(jnp.int32, (1, wide), 1)
         s = jnp.where(position < lengths[cl, m], s * scale2, NEG)
-        before = m_st[nth][:, :1]
+        before = m_st[nth, at, :1]
         top = jnp.maximum(before, jnp.max(s, axis=1, keepdims=True))
         keep = jnp.exp2(before - top)
         w = jnp.exp2(s - top)
-        m_st[nth] = jnp.broadcast_to(top, (2 * rows, 128))
-        l_st[nth] = l_st[nth] * keep + jnp.sum(w, axis=1, keepdims=True)
-        acc[nth] = acc[nth] * keep + lax.dot_general(w.astype(jnp.bfloat16), keys[:latent, :], nt,
-                                                     preferred_element_type=jnp.float32)
+        m_st[nth, at] = jnp.broadcast_to(top, ((end - begin) * rows, 128))
+        l_st[nth, at] = l_st[nth, at] * keep + jnp.sum(w, axis=1, keepdims=True)
+        acc[nth, at] = acc[nth, at] * keep + lax.dot_general(w.astype(jnp.bfloat16), keys[:latent, columns], nt,
+                                                             preferred_element_type=jnp.float32)
 
     ocount = [0]
 
-    def close_block(cl, m, nth):
+    def close_block(cl, m, nth, pieces=(0, 1)):
         rel = rels[nth]
         sl, k = cl * per + m, cl * two + 2 * m + role
         back = (n_ctx - rel) % n_ctx
-        norm = l_st[nth][:, :1]
-        live = norm > 0.0
-        safe = jnp.where(live, norm, 1.0)
-        o = (acc[nth] * (1.0 / safe)).astype(jnp.bfloat16)
-        norm = l_st[nth]
-        lse = jnp.where(norm > 0.0, m_st[nth] + jnp.log2(jnp.where(norm > 0.0, norm, 1.0)), NEG)
-        for rr in (0, 1):
-            piece = o[rr * rows:(rr + 1) * rows]
-            e = lse[rr * rows:(rr + 1) * rows].T[:8]
+        for rr in pieces:
+            at = slice(rr * rows, (rr + 1) * rows)
+            norm = l_st[nth, at]
+            live = norm > 0.0
+            safe = jnp.where(live, norm, 1.0)
+            piece = (acc[nth, at] * (1.0 / safe[:, :1])).astype(jnp.bfloat16)
+            e = jnp.where(live, m_st[nth, at] + jnp.log2(safe), NEG).T[:8]
             if rel == 0 and rr == 0:
                 o_in[k, 0] = piece
                 e_in[k, 0] = e
                 continue
             o_out[sl, rel * 2 + rr] = piece
             e_out[sl, rel * 2 + rr] = e
-        for rr in (0, 1):
+        for rr in pieces:
             if rel == 0 and rr == 0:
                 continue
             dev = (role_at(rr), ctx_at(rel), req)
@@ -389,10 +400,23 @@
 
     def last_part(cl, m, p):
         p = jnp.int32(p)
-        await_part(cl, m, p)
-        for nth in range(n_ctx):
-            part(cl, m, p, nth)
-            close_block(cl, m, nth)
+        if cl:
+            await_part(cl, m, p)
+            for nth in range(n_ctx):
+                part(cl, m, p, nth)
+                close_block(cl, m, nth)
+            return
+        for c in range(cuts):
+            sample = k_ref(cl, m, 0).at[pl.ds(0, half), pl.ds(0, width)]
+            arrived(sample, k_sem(cl, m, 3 + c, role))
+            arrived(sample, k_sem(cl, m, 3 + c, other))
+            for nth in range(n_ctx):
+                if c < cuts - 1:
+                    part(cl, m, p, nth, 0, 2, c * width, width)
+                    continue
+                for rr in ((1, 0) if rels[nth] else (0, 1)):
+                    part(cl, m, p, nth, rr, rr + 1, c * width, width)
+                    close_block(cl, m, nth, (rr,))
 
     out_rows = lax.broadcasted_iota(jnp.int32, (two * block, 128), 0)
     which = lax.div(lax.rem(out_rows, block), steps)
@@ -430,7 +454,7 @@
                 att_out[cl * two + k, pl.ds(r0, block), :] = res[k * block:(k + 1) * block]
             return carry
 
-        lax.fori_loop(0, heads // BLOCK_HEADS, up, 0, unroll=UNROLL)
+        lax.fori_loop(0, heads // BLOCK_HEADS, up, 0, unroll=min(UNROLL, heads // BLOCK_HEADS))
         for k in range(two):
             e = cl * two + k
             owner = owner_of(cl, jnp.int32(k), req)
@@ -569,7 +593,7 @@
             dma((3 * high, 2)),
             dma((3 * two, 2)),
             dma((chunks, 2)),
-            dma((per, 4, 2)),
+            dma((per, 5, 2)),
             dma((2 * per, 2, 2)),
             dma((3 * two * n_ctx, 2)),
             dma((3 * per, groups, 2)),

time: 64.2 us -> 63.1 us (0.983); the launches traced: 64.1 us -> 62.3 us
  Pallas kernels: 63.4 us -> 61.7 us
    pallas_call x1, Pallas kernels: 63.4 us -> 61.7 us  [shards(): pl.pallas_call(functools.partial(kernel, (n_req, n_ctx, scale2)), out_sha...]
where the time goes in v3:
time: 63.1 us; the launch traced here: 62.3 us
  Pallas kernels  61.7 us (98%)
    pallas_call x1, Pallas kernels, shards(): pl.pallas_call(functools.partial(kernel, (n_req, n_ctx, scale2)), out_sha...  61.7 us

profile of v3, /device:TPU:0, one launch (start us, length us, event | category | flops | bytes accessed | tf_op | source)
XLA Modules:
  0.0 62.3 jit_solution(12904961020049737733)
XLA Ops:
  0.0 61.7 %shard_map.82 = bf16[2,4,4096]{2,1,0:T(4,128)(2,1)S(1)} custom-call(s32[16]{0:T(128)} %slot_ref.1, s32[16]{0:T(128)} %len_ref.1, bf16[16,288,512]{2,1,0:T(8,128)(2,1)} %bitcast.1, bf16[2,4,4096]{2,1,0:T(4,128)(2,1)} %qn_any.1, bf16[2,4,2048]{2,1,0:T(4,128)(2,1)} %qr_any.1, bf16[2,4,576]{2,1,0:T(4,128)(2,1)} %new_any.1, bf16[32,128,512]{2,1,0:T(8,128)(2,1)} %wk_ref.1, ...), custom_call_target="tpu_custom_call" | custom-call | tf_op jit(solution)/shard_map/pallas_call | solution.py:551
  61.7 0.6 %copy.10 = bf16[2,4,4096]{2,1,0:T(4,128)(2,1)} copy(bf16[2,4,4096]{2,1,0:T(4,128)(2,1)S(1)} %shard_map.82) | data formatting | bytes 131072
